TPU v7x, 128 devices: a whole 4x4x4 slice. The times are simulated.
128 devices in a mesh: row: 8 (over x, core), col: 16 (over z, y).
Axes of the slice: x: 4, y: 4, z: 4, core: 2. Of those that a mesh axis runs over, the one named last changes fastest.
Arguments:
- basis: bfloat16 [1152, 256, 128], P(('row', 'col')), may hold values from -1.5 to 1.5
- row_index: int32 [1152, 128], P(('row', 'col')), may hold values from 0 to 255
- group_slot: int32 [1152], P(('row', 'col')), may hold values from 0 to 1535, as said below
- x_blocks: bfloat16 [96, 256, 256], P('row', 'col')
- zinv_blocks: bfloat16 [96, 256, 256], P('row', 'col')
Outputs:
- schur_tiles: float32 [96, 2048, 2048], P('row', None, 'col')
Inputs may be any that keep to these rules, and one draw needn't show every extreme that they name: Values are distinct; group_slot // 16 is the group's PSD block and group_slot % 16 its position there. A group stored on the device at (row index a, col index c) has its position among c * 1 to c + 1 - 1. Of the groups of one device, at most 2 belong to blocks of one index of row (blocks b with b // 12 equal to it), and every device reaches 2 for some index. The positions that the blocks of one index of row have on one index of col hold exactly 9 groups.
All inputs are finite; a program needn't handle non-finite values.
Results may differ from a plain program's by a relative error of at most 0.00048.
Values may be sent and summed in bfloat16 or wider, within the bound.
A program may use at most 192 MiB of HBM per device.

v0:
```python
import jax
import jax.numpy as jnp
from jax import lax
from jax.sharding import PartitionSpec as P

GMAX = 16


def sent_together(arrays, axis, split_dim, concat_dim, along):
    columns = [a.reshape(*a.shape[:along], -1) for a in arrays]
    both = jnp.concatenate(columns, axis=along)
    result, at, done = (
        lax.all_to_all(both, axis, split_axis=split_dim, concat_axis=concat_dim, tiled=True),
        0,
        [],
    )
    for a, column in zip(arrays, columns):
        slab = result[..., at : at + column.shape[along]]
        done.append(slab.reshape(*slab.shape[:along], *a.shape[along:]))
        at += column.shape[along]
    return tuple(done)


def side_by_side(arrays, axis, dim, along):
    widths = [a.shape[along] for a in arrays]
    both = jnp.concatenate(arrays, axis=along)
    result = lax.all_gather(both, axis, axis=dim, tiled=True)
    return tuple(jnp.split(result, [sum(widths[:k]) for k in range(1, len(widths))], axis=along))


def place_rows(selector, values):
    flat_values = values.reshape(values.shape[0], -1)
    moved_rows = jnp.dot(selector, flat_values, preferred_element_type=jnp.float32)
    return moved_rows.astype(values.dtype).reshape((selector.shape[0],) + values.shape[1:])


def place_ints(selector, values):
    moved_rows = jnp.dot(selector, values, preferred_element_type=jnp.int32)
    return moved_rows


def pair_tiles(members):
    stacked, x_full, z_full, rows_all, mask_all, near_basis, near_rows, near_mask = members
    group_width = near_basis.shape[-1]
    order = x_full.shape[0]
    positions = rows_all.shape[0]
    order_ids = jnp.arange(order, dtype=jnp.int32)
    row_pick = (rows_all.reshape(-1)[:, None] == order_ids[None, :]).astype(jnp.bfloat16)
    x_rows = (
        jnp.dot(row_pick, x_full, preferred_element_type=jnp.float32)
        .astype(jnp.bfloat16)
        .reshape(positions, group_width, order)
    )
    z_rows = (
        jnp.dot(row_pick, z_full, preferred_element_type=jnp.float32)
        .astype(jnp.bfloat16)
        .reshape(positions, group_width, order)
    )
    images = jnp.concatenate([stacked[:, 0], x_rows, stacked[:, 1], z_rows], axis=1)
    products = jnp.einsum("pcn,snk->pcsk", images, near_basis, preferred_element_type=jnp.float32)
    products = products.reshape(products.shape[0], products.shape[1], -1)
    column_pick = (order_ids[:, None] == near_rows.reshape(-1)[None, :]).astype(jnp.bfloat16)
    picked = jnp.einsum("pcn,nk->pck", images, column_pick, preferred_element_type=jnp.float32)
    upper = 2 * group_width
    third = 3 * group_width
    tile_sum = (
        products[:, group_width:upper] * picked[:, upper:third]
        + picked[:, group_width:upper] * products[:, upper:third]
    )
    tile_sum = (
        tile_sum
        + products[:, :group_width] * picked[:, third:]
        + picked[:, :group_width] * products[:, third:]
    )
    row_mask = mask_all.astype(jnp.float32)
    column_mask = jnp.repeat(near_mask.astype(jnp.float32), group_width)
    tile_sum = tile_sum * row_mask[:, None, None] * column_mask[None, None, :]
    return tile_sum.reshape(-1, tile_sum.shape[2])


def body(basis, row_index, group_slot, x_blocks, zinv_blocks):
    row_count = lax.axis_size("row")
    col_count = lax.axis_size("col")
    my_row = lax.axis_index("row")
    my_col = lax.axis_index("col")
    groups = basis.shape[0]
    owned = x_blocks.shape[0]
    places = GMAX // col_count
    capacity = (groups + row_count - 1) // row_count
    slot_count = row_count * capacity
    block_of = group_slot // GMAX
    owner_of = block_of // owned
    same_owner = (owner_of[:, None] == owner_of[None, :]).astype(jnp.int32)
    earlier = jnp.sum(jnp.tril(same_owner, -1), axis=1)
    target = owner_of * capacity + earlier
    choose = target[None, :] == jnp.arange(slot_count, dtype=jnp.int32)[:, None]
    send_basis = place_rows(choose.astype(jnp.bfloat16), basis)
    send_rows = place_ints(choose.astype(jnp.int32), row_index)
    send_slot = place_ints(choose.astype(jnp.int32), (group_slot + 1)[:, None])[:, 0] - 1
    got_basis, got_rows, got_slot = (
        lax.all_to_all(send_basis, "row", split_axis=0, concat_axis=0, tiled=True),
        *sent_together((send_rows, send_slot), "row", 0, 0, 1),
    )
    is_valid = got_slot >= 0
    spot_index = (got_slot // GMAX - my_row * owned) * places + (got_slot % GMAX - my_col * places)
    settle = (
        spot_index[None, :] == jnp.arange(owned * places, dtype=jnp.int32)[:, None]
    ) & is_valid[None, :]
    near_basis = place_rows(settle.astype(jnp.bfloat16), got_basis)
    near_basis = near_basis.reshape((owned, places) + near_basis.shape[1:])
    near_rows = place_ints(settle.astype(jnp.int32), got_rows).reshape(owned, places, -1)
    near_mask = (
        jnp.sum(settle.astype(jnp.float32), axis=1).astype(jnp.bfloat16).reshape(owned, places)
    )
    x_full, z_full, all_basis, rows_all, mask_all = (
        *side_by_side((x_blocks, zinv_blocks), "col", 1, 0),
        lax.all_gather(near_basis, "col", axis=1, tiled=True),
        lax.all_gather(near_rows, "col", axis=1, tiled=True),
        lax.all_gather(near_mask, "col", axis=1, tiled=True),
    )
    all_x = jnp.einsum(
        "jpnc,jnm->jpcm", all_basis, x_full, preferred_element_type=jnp.float32
    ).astype(jnp.bfloat16)
    all_z = jnp.einsum(
        "jpnc,jnm->jpcm", all_basis, z_full, preferred_element_type=jnp.float32
    ).astype(jnp.bfloat16)
    stacked = jnp.stack([all_x, all_z], axis=2)
    tile_blocks = lax.map(
        pair_tiles, (stacked, x_full, z_full, rows_all, mask_all, near_basis, near_rows, near_mask)
    )
    return tile_blocks


def solution(mesh):
    placed = (
        P(("row", "col"), None, None),
        P(("row", "col"), None),
        P(("row", "col")),
        P("row", "col", None),
        P("row", "col", None),
    )
    return jax.shard_map(
        body, mesh=mesh, in_specs=placed, out_specs=P("row", None, "col"), check_vma=False
    )
```

profile of v0, /device:TPU:1, one launch (start us, length us, event | category | flops | bytes accessed | tf_op | source)
XLA Modules:
  0.0 411.3 jit_solution(17968727844061814337)
XLA Ops:
  10.7 5.8 %all-to-all-start = ((s32[8,2,129]{2,1,0:T(2,128)}), s32[8,2,129]{2,1,0:T(2,128)S(1)}, u32[]{:S(2)}, u32[]{:S(2)}) async-start(s32[8,2,129]{2,1,0:T(2,128)} %pad_add_fusion), calls=%async_computation | async-start | bytes 32768 | tf_op jit(solution)/shard_map/all_to_all | solution.py:13
  21.2 4.2 %all-to-all-start.1 = ((bf16[16,256,128]{2,1,0:T(8,128)(2,1)}), bf16[16,256,128]{2,1,0:T(8,128)(2,1)S(1)}, u32[]{:S(2)}, u32[]{:S(2)}) async-start(bf16[16,256,128]{2,1,0:T(8,128)(2,1)} %bitcast.45), calls=%async_computation.1 | async-start | bytes 2097152 | tf_op jit(solution)/shard_map/all_to_all | solution.py:101
  25.5 14.8 %all-to-all-done.1 = bf16[16,256,128]{2,1,0:T(8,128)(2,1)S(1)} async-done(((bf16[16,256,128]{2,1,0:T(8,128)(2,1)}), bf16[16,256,128]{2,1,0:T(8,128)(2,1)S(1)}, u32[]{:S(2)}, u32[]{:S(2)}) %all-to-all-start.1) | async-done | bytes 1048608 | tf_op jit(solution)/shard_map/all_to_all | solution.py:101
  43.9 21.8 %all-gather = s32[12,2048]{1,0:T(8,128)S(1)} all-gather(s32[12,128]{1,0:T(8,128)S(1)} %fusion.32), channel_id=2, replica_groups=mesh['row'=8,'col'=16] {'col'}, dimensions={1}, use_global_device_ids=true | all-gather | bytes 104448 | tf_op jit(solution)/shard_map/all_gather | solution.py:118
  65.9 16.1 %all-gather.1 = bf16[16,1,12]{2,1,0:T(2,128)(2,1)S(1)} all-gather(bf16[1,1,12]{2,1,0:T(2,128)(2,1)S(1)} %bitcast.137), channel_id=1, replica_groups=mesh['row'=8,'col'=16] {'col'}, dimensions={0}, use_global_device_ids=true | all-gather | bytes 408 | tf_op jit(solution)/shard_map/all_gather | solution.py:119
  85.4 71.0 %all-gather.5.cloned.1.call-done = bf16[12,16,256,128]{2,3,1,0:T(8,128)(2,1)} async-done(((bf16[12,1,256,128]{2,3,1,0:T(8,128)(2,1)}), bf16[12,16,256,128]{2,3,1,0:T(8,128)(2,1)}) %all-gather.5.cloned.1.call-update) | async-done | bytes 12582928 | tf_op jit(solution)/shard_map/all_gather | solution.py:117
  156.4 11.4 %convert_bitcast_fusion = bf16[12,16,1,128,256]{4,3,1,0,2:T(8,128)(2,1)} fusion(bf16[12,16,256,128]{2,3,1,0:T(8,128)(2,1)} %all-gather.5.cloned.1.call-done, bf16[24,256,256]{2,1,0:T(8,128)(2,1)} %all-gather.7.cloned.1.call-done), kind=kOutput, calls=%fused_computation.45 | convolution fusion | flops 3227516928 | bytes 26738688 | tf_op jit(solution)/shard_map/jpnc,jnm->jpcm/dot_general | solution.py:124
  169.4 7.7 %convert_bitcast_fusion.1 = bf16[12,16,1,128,256]{4,3,1,0,2:T(8,128)(2,1)} fusion(bf16[12,16,256,128]{2,3,1,0:T(8,128)(2,1)S(1)} %copy-done.2, bf16[24,256,256]{2,1,0:T(8,128)(2,1)} %all-gather.7.cloned.1.call-done), kind=kOutput, calls=%fused_computation.46 | convolution fusion | flops 3227516928 | bytes 26738688 | tf_op jit(solution)/shard_map/jpnc,jnm->jpcm/dot_general | solution.py:121
  177.1 20.5 %pad_maximum_fusion.3 = bf16[12,16,2,128,256]{4,3,1,0,2:T(8,128)(2,1)} fusion(bf16[12,16,1,128,256]{4,3,1,0,2:T(8,128)(2,1)} %convert_bitcast_fusion, bf16[12,16,1,128,256]{4,3,1,0,2:T(8,128)(2,1)} %convert_bitcast_fusion.1), kind=kLoop, calls=%fused_computation.44 | loop fusion | flops 12582912 | bytes 50331648 | tf_op jit(solution)/shard_map/stack | solution.py:127
  197.7 206.1 %while.10 = (s32[]{:T(128)}, f32[12,2048,128]{2,1,0:T(8,128)}, bf16[12,16,2,128,256]{4,3,1,0,2:T(8,128)(2,1)}, s32[12,16,128]{2,1,0:T(8,128)S(1)}, bf16[12,256,2...) while((s32[]{:T(128)}, f32[12,2048,128]{2,1,0:T(8,128)}, ...), condition=%wide.region_3.4_spmd, body=%wide.region_2.3_spmd.sunk | while | flops 1648656384 | bytes 39161136 | solution.py:128
  204.7 3.6 fusion.70
  209.4 4.4 %fusion.74 = f32[16,128,128]{2,1,0:T(8,128)S(1)} fusion(f32[16,512,128]{2,1,0:T(8,128)} %fusion.70, f32[16,512,128]{2,1,0:T(8,128)} %fusion.72, f32[]{:T(128)S(6)} %convert.11, f32[16]{0:T(128)S(1)} %fusion.73), kind=kLoop, calls=%fused_computation.8.clone.1 | loop fusion | flops 2359296 | bytes 9437252 | tf_op jit(solution)/shard_map/while/body/eval_jaxpr/mul | solution.py:77
  221.9 3.6 fusion.70
  226.6 4.4 %fusion.74 = f32[16,128,128]{2,1,0:T(8,128)S(1)} fusion(f32[16,512,128]{2,1,0:T(8,128)} %fusion.70, f32[16,512,128]{2,1,0:T(8,128)} %fusion.72, f32[]{:T(128)S(6)} %convert.11, f32[16]{0:T(128)S(1)} %fusion.73), kind=kLoop, calls=%fused_computation.8.clone.1 | loop fusion | flops 2359296 | bytes 9437252 | tf_op jit(solution)/shard_map/while/body/eval_jaxpr/mul | solution.py:77
  239.1 3.6 fusion.70
  243.8 4.4 %fusion.74 = f32[16,128,128]{2,1,0:T(8,128)S(1)} fusion(f32[16,512,128]{2,1,0:T(8,128)} %fusion.70, f32[16,512,128]{2,1,0:T(8,128)} %fusion.72, f32[]{:T(128)S(6)} %convert.11, f32[16]{0:T(128)S(1)} %fusion.73), kind=kLoop, calls=%fused_computation.8.clone.1 | loop fusion | flops 2359296 | bytes 9437252 | tf_op jit(solution)/shard_map/while/body/eval_jaxpr/mul | solution.py:77
  256.2 3.6 fusion.70
  261.0 4.4 %fusion.74 = f32[16,128,128]{2,1,0:T(8,128)S(1)} fusion(f32[16,512,128]{2,1,0:T(8,128)} %fusion.70, f32[16,512,128]{2,1,0:T(8,128)} %fusion.72, f32[]{:T(128)S(6)} %convert.11, f32[16]{0:T(128)S(1)} %fusion.73), kind=kLoop, calls=%fused_computation.8.clone.1 | loop fusion | flops 2359296 | bytes 9437252 | tf_op jit(solution)/shard_map/while/body/eval_jaxpr/mul | solution.py:77
  273.4 3.6 fusion.70
  278.1 4.4 %fusion.74 = f32[16,128,128]{2,1,0:T(8,128)S(1)} fusion(f32[16,512,128]{2,1,0:T(8,128)} %fusion.70, f32[16,512,128]{2,1,0:T(8,128)} %fusion.72, f32[]{:T(128)S(6)} %convert.11, f32[16]{0:T(128)S(1)} %fusion.73), kind=kLoop, calls=%fused_computation.8.clone.1 | loop fusion | flops 2359296 | bytes 9437252 | tf_op jit(solution)/shard_map/while/body/eval_jaxpr/mul | solution.py:77
  290.6 3.6 fusion.70
  295.3 4.4 %fusion.74 = f32[16,128,128]{2,1,0:T(8,128)S(1)} fusion(f32[16,512,128]{2,1,0:T(8,128)} %fusion.70, f32[16,512,128]{2,1,0:T(8,128)} %fusion.72, f32[]{:T(128)S(6)} %convert.11, f32[16]{0:T(128)S(1)} %fusion.73), kind=kLoop, calls=%fused_computation.8.clone.1 | loop fusion | flops 2359296 | bytes 9437252 | tf_op jit(solution)/shard_map/while/body/eval_jaxpr/mul | solution.py:77
  307.8 3.6 fusion.70
  312.5 4.4 %fusion.74 = f32[16,128,128]{2,1,0:T(8,128)S(1)} fusion(f32[16,512,128]{2,1,0:T(8,128)} %fusion.70, f32[16,512,128]{2,1,0:T(8,128)} %fusion.72, f32[]{:T(128)S(6)} %convert.11, f32[16]{0:T(128)S(1)} %fusion.73), kind=kLoop, calls=%fused_computation.8.clone.1 | loop fusion | flops 2359296 | bytes 9437252 | tf_op jit(solution)/shard_map/while/body/eval_jaxpr/mul | solution.py:77
  325.0 3.6 fusion.70
  329.7 4.4 %fusion.74 = f32[16,128,128]{2,1,0:T(8,128)S(1)} fusion(f32[16,512,128]{2,1,0:T(8,128)} %fusion.70, f32[16,512,128]{2,1,0:T(8,128)} %fusion.72, f32[]{:T(128)S(6)} %convert.11, f32[16]{0:T(128)S(1)} %fusion.73), kind=kLoop, calls=%fused_computation.8.clone.1 | loop fusion | flops 2359296 | bytes 9437252 | tf_op jit(solution)/shard_map/while/body/eval_jaxpr/mul | solution.py:77
  342.1 3.6 fusion.70
  346.9 4.4 %fusion.74 = f32[16,128,128]{2,1,0:T(8,128)S(1)} fusion(f32[16,512,128]{2,1,0:T(8,128)} %fusion.70, f32[16,512,128]{2,1,0:T(8,128)} %fusion.72, f32[]{:T(128)S(6)} %convert.11, f32[16]{0:T(128)S(1)} %fusion.73), kind=kLoop, calls=%fused_computation.8.clone.1 | loop fusion | flops 2359296 | bytes 9437252 | tf_op jit(solution)/shard_map/while/body/eval_jaxpr/mul | solution.py:77
  364.0 4.4 %fusion.74 = f32[16,128,128]{2,1,0:T(8,128)S(1)} fusion(f32[16,512,128]{2,1,0:T(8,128)} %fusion.70, f32[16,512,128]{2,1,0:T(8,128)} %fusion.72, f32[]{:T(128)S(6)} %convert.11, f32[16]{0:T(128)S(1)} %fusion.73), kind=kLoop, calls=%fused_computation.8.clone.1 | loop fusion | flops 2359296 | bytes 9437252 | tf_op jit(solution)/shard_map/while/body/eval_jaxpr/mul | solution.py:77
  376.5 3.6 fusion.70
  381.2 4.4 %fusion.74 = f32[16,128,128]{2,1,0:T(8,128)S(1)} fusion(f32[16,512,128]{2,1,0:T(8,128)} %fusion.70, f32[16,512,128]{2,1,0:T(8,128)} %fusion.72, f32[]{:T(128)S(6)} %convert.11, f32[16]{0:T(128)S(1)} %fusion.73), kind=kLoop, calls=%fused_computation.8.clone.1 | loop fusion | flops 2359296 | bytes 9437252 | tf_op jit(solution)/shard_map/while/body/eval_jaxpr/mul | solution.py:77
  398.4 4.4 %fusion.74 = f32[16,128,128]{2,1,0:T(8,128)S(1)} fusion(f32[16,512,128]{2,1,0:T(8,128)} %fusion.70, f32[16,512,128]{2,1,0:T(8,128)} %fusion.72, f32[]{:T(128)S(6)} %convert.11, f32[16]{0:T(128)S(1)} %fusion.73), kind=kLoop, calls=%fused_computation.8.clone.1 | loop fusion | flops 2359296 | bytes 9437252 | tf_op jit(solution)/shard_map/while/body/eval_jaxpr/mul | solution.py:77
  (161 shorter events, 129.1 us)
Async XLA Ops:
  6.5 3.4 copy-start
  6.5 75.5 %all-gather.7.cloned.1.call-start = ((), (), s32[]{:S(2)}) async-start(), calls=%async_computation.3 | async-start | bytes 3342336 | tf_op jit(solution)/shard_map/all_gather | solution.py:27
  10.7 10.4 %all-to-all-start = ((s32[8,2,129]{2,1,0:T(2,128)}), s32[8,2,129]{2,1,0:T(2,128)S(1)}, u32[]{:S(2)}, u32[]{:S(2)}) async-start(s32[8,2,129]{2,1,0:T(2,128)} %pad_add_fusion), calls=%async_computation | async-start | bytes 32768 | tf_op jit(solution)/shard_map/all_to_all | solution.py:13
  21.2 19.2 %all-to-all-start.1 = ((bf16[16,256,128]{2,1,0:T(8,128)(2,1)}), bf16[16,256,128]{2,1,0:T(8,128)(2,1)S(1)}, u32[]{:S(2)}, u32[]{:S(2)}) async-start(bf16[16,256,128]{2,1,0:T(8,128)(2,1)} %bitcast.45), calls=%async_computation.1 | async-start | bytes 2097152 | tf_op jit(solution)/shard_map/all_to_all | solution.py:101
  25.3 131.0 %all-gather.5.cloned.1.call-start = ((), (), s32[]{:S(2)}) async-start(), calls=%async_computation.2 | async-start | bytes 13369344 | tf_op jit(solution)/shard_map/all_gather | solution.py:117
  156.4 13.0 %copy-start.2 = (bf16[12,16,256,128]{2,3,1,0:T(8,128)(2,1)S(1)}, bf16[12,16,256,128]{2,3,1,0:T(8,128)(2,1)}, u32[]{:S(2)}) copy-start(bf16[12,16,256,128]{2,3,1,0:T(8,128)(2,1)} %all-gather.5.cloned.1.call-done) | copy-start | bytes 37748740
  403.8 0.7 copy-start.1
Sparse Core Ops, SparseCore 0:
  9.4 54.1 all-gather.6
  65.8 90.5 all-gather.4
where the time goes:
time: 413 us; the launch traced here: 411 us
  matrix products  126 us (31%)
  waiting for transfers between devices  87.1 us (21%)
  other arithmetic  76.2 us (18%)
  local copies, waits for them, and re-layouts  53.5 us (13%)
  blocking collectives  37.9 us (9%)
  between operations  13.5 us (3%)
  starting transfers between devices  9.97 us (2%)
  loops' own time  7.33 us (2%)
    all_gather x1, waiting for transfers between devices, body(): lax.all_gather(near_basis, 'col', axis=1, tiled=True)  71 us
    mul x12, other arithmetic, pair_tiles(): tile_sum = tile_sum * row_mask[:, None, None] * column_mask[None, None, :]  52.3 us
    dot_general x12, matrix products, pair_tiles(): jnp.einsum('pcn,snk->pcsk', images, near_basis, preferred_element_type=jn...  43 us
    dot_general x12, matrix products, pair_tiles(): jnp.einsum('pcn,nk->pck', images, column_pick, preferred_element_type=jnp...  32.7 us
    all_gather x1, blocking collectives, body(): lax.all_gather(near_rows, 'col', axis=1, tiled=True)  21.8 us
    squeeze x12, local copies, waits for them, and re-layouts, body(): lax.map(pair_tiles, (stacked, x_full, z_full, rows_all, mask_all, near_ba...  20.8 us
    another operation x1, other arithmetic, body(): stacked = jnp.stack([all_x, all_z], axis=2)  20.5 us
    dot_general x12, matrix products, pair_tiles(): jnp.dot(row_pick, x_full, preferred_element_type=jnp.float32)  20 us
  transfers between devices with their start and end apart: 4, of which 3 were waited for; matrix products, arithmetic and copies ran while one was open for 3% of the time, Pallas kernels for 0%

commit v1 on v0

--- a/solution.py
+++ b/solution.py
@@ -114,7 +114,9 @@
     )
     x_full, z_full, all_basis, rows_all, mask_all = (
         *side_by_side((x_blocks, zinv_blocks), "col", 1, 0),
-        lax.all_gather(near_basis, "col", axis=1, tiled=True),
+        jnp.concatenate(
+            lax.all_to_all(jnp.stack([near_basis] * lax.axis_size("col")), "col", 0, 0), axis=1
+        ),
         lax.all_gather(near_rows, "col", axis=1, tiled=True),
         lax.all_gather(near_mask, "col", axis=1, tiled=True),
     )

time: 413 us -> 561 us (1.36); the launches traced: 411 us -> 550 us
  blocking collectives: 37.9 us -> 225 us
  waiting for transfers between devices: 87.1 us -> 16.1 us
  matrix products: 126 us -> 136 us
  starting transfers between devices: 9.97 us -> 17.9 us
    all_gather x1, blocking collectives: 21.8 us -> 210 us  [body(): lax.all_gather(near_rows, 'col', axis=1, tiled=True)]
    all_gather x1 -> x0, waiting for transfers between devices: 71 us -> none  [body(): lax.all_gather(near_basis, 'col', axis=1, tiled=True)]
    dot_general x12, matrix products: 8.84 us -> 19.7 us  [pair_tiles(): jnp.dot(row_pick, z_full, preferred_element_type=jnp.float32)]
    all_to_all x0 -> x1, starting transfers between devices: none -> 7.94 us  [body(): lax.all_to_all(jnp.stack([near_basis] * lax.axis_size('col')), 'col', 0, 0)]
  transfers between devices with their start and end apart: 4 -> 4, of which waited for: 3 -> 2; matrix products, arithmetic and copies ran while one was open for 3% -> 2% of each run, Pallas kernels for 0% -> 0%
where the time goes in v1:
time: 561 us; the launch traced here: 550 us
  blocking collectives  225 us (40%)
  matrix products  136 us (24%)
  other arithmetic  75.3 us (13%)
  local copies, waits for them, and re-layouts  58.4 us (10%)
  starting transfers between devices  17.9 us (3%)
  waiting for transfers between devices  16.1 us (3%)
  between operations  13.5 us (2%)
  loops' own time  8.38 us (1%)
    all_gather x1, blocking collectives, body(): lax.all_gather(near_rows, 'col', axis=1, tiled=True)  210 us
    mul x12, other arithmetic, pair_tiles(): tile_sum = tile_sum * row_mask[:, None, None] * column_mask[None, None, :]  52.3 us
    dot_general x12, matrix products, pair_tiles(): jnp.einsum('pcn,snk->pcsk', images, near_basis, preferred_element_type=jn...  42.9 us
    dot_general x12, matrix products, pair_tiles(): jnp.einsum('pcn,nk->pck', images, column_pick, preferred_element_type=jnp...  32.8 us
    squeeze x12, local copies, waits for them, and re-layouts, body(): lax.map(pair_tiles, (stacked, x_full, z_full, rows_all, mask_all, near_ba...  20.8 us
    another operation x1, other arithmetic, body(): stacked = jnp.stack([all_x, all_z], axis=2)  20.6 us
    dot_general x12, matrix products, pair_tiles(): jnp.dot(row_pick, x_full, preferred_element_type=jnp.float32)  20 us
    dot_general x12, matrix products, pair_tiles(): jnp.dot(row_pick, z_full, preferred_element_type=jnp.float32)  19.7 us
  transfers between devices with their start and end apart: 4, of which 2 were waited for; matrix products, arithmetic and copies ran while one was open for 2% of the time, Pallas kernels for 0%

profile of v1, /device:TPU:1, one launch (start us, length us, event | category | flops | bytes accessed | tf_op | source)
XLA Modules:
  0.0 550.0 jit_solution(15259061172466822604)
XLA Ops:
  9.1 5.8 %all-to-all-start = ((s32[8,2,129]{2,1,0:T(2,128)}), s32[8,2,129]{2,1,0:T(2,128)S(1)}, u32[]{:S(2)}, u32[]{:S(2)}) async-start(s32[8,2,129]{2,1,0:T(2,128)} %pad_add_fusion), calls=%async_computation | async-start | bytes 32768 | tf_op jit(solution)/shard_map/all_to_all | solution.py:13
  19.5 4.2 all-to-all-start.1
  23.8 14.8 %all-to-all-done.1 = bf16[16,256,128]{2,1,0:T(8,128)(2,1)S(1)} async-done(((bf16[16,256,128]{2,1,0:T(8,128)(2,1)}), bf16[16,256,128]{2,1,0:T(8,128)(2,1)S(1)}, u32[]{:S(2)}, u32[]{:S(2)}) %all-to-all-start.1) | async-done | bytes 1048608 | tf_op jit(solution)/shard_map/all_to_all | solution.py:101
  41.2 6.1 %stack.12 = bf16[16,12,1,256,128]{3,4,1,2,0:T(8,128)(2,1)} broadcast(bf16[12,256,128]{1,2,0:T(8,128)(2,1)S(1)} %copy.33), dimensions={1,3,4} | broadcast | bytes 13369344 | tf_op jit(solution)/shard_map/stack | solution.py:118
  47.3 7.9 %all-to-all-start.2 = ((bf16[16,12,1,256,128]{3,4,1,2,0:T(8,128)(2,1)}), bf16[16,12,1,256,128]{3,4,1,2,0:T(8,128)(2,1)}, u32[]{:S(2)}, u32[]{:S(2)}) async-start(bf16[16,12,1,256,128]{3,4,1,2,0:T(8,128)(2,1)} %stack.12), calls=%async_computation.2 | async-start | bytes 25165824 | tf_op jit(solution)/shard_map/all_to_all | solution.py:118
  56.2 209.8 %all-gather = s32[12,2048]{1,0:T(8,128)S(1)} all-gather(s32[12,128]{1,0:T(8,128)S(1)} %fusion.42), channel_id=2, replica_groups=mesh['row'=8,'col'=16] {'col'}, dimensions={1}, use_global_device_ids=true | all-gather | bytes 104448 | tf_op jit(solution)/shard_map/all_gather | solution.py:120
  266.1 14.8 %all-gather.1 = bf16[16,1,12]{2,1,0:T(2,128)(2,1)S(1)} all-gather(bf16[1,1,12]{2,1,0:T(2,128)(2,1)S(1)} %bitcast.147), channel_id=1, replica_groups=mesh['row'=8,'col'=16] {'col'}, dimensions={0}, use_global_device_ids=true | all-gather | bytes 408 | tf_op jit(solution)/shard_map/all_gather | solution.py:121
  281.0 4.0 fusion.61
  284.9 9.2 %convert_bitcast_fusion = bf16[12,16,1,128,256]{4,3,1,0,2:T(8,128)(2,1)} fusion(bf16[16,12,1,256,128]{3,4,1,2,0:T(8,128)(2,1)} %all-to-all-done.2, bf16[24,256,256]{2,1,0:T(8,128)(2,1)S(1)} %copy-done.2), kind=kOutput, calls=%fused_computation.49 | convolution fusion | flops 3227516928 | bytes 26738688 | tf_op jit(solution)/shard_map/jpnc,jnm->jpcm/dot_general | solution.py:126
  294.1 9.1 %convert_bitcast_fusion.1 = bf16[12,16,1,128,256]{4,3,1,0,2:T(8,128)(2,1)} fusion(bf16[16,12,1,256,128]{3,4,1,2,0:T(8,128)(2,1)} %all-to-all-done.2, bf16[24,256,256]{2,1,0:T(8,128)(2,1)S(1)} %copy-done.2), kind=kOutput, calls=%fused_computation.50 | convolution fusion | flops 3227516928 | bytes 26738688 | tf_op jit(solution)/shard_map/jpnc,jnm->jpcm/dot_general | solution.py:123
  303.2 20.6 %pad_maximum_fusion.3 = bf16[12,16,2,128,256]{4,3,1,0,2:T(8,128)(2,1)} fusion(bf16[12,16,1,128,256]{4,3,1,0,2:T(8,128)(2,1)} %convert_bitcast_fusion, bf16[12,16,1,128,256]{4,3,1,0,2:T(8,128)(2,1)} %convert_bitcast_fusion.1), kind=kLoop, calls=%fused_computation.44 | loop fusion | flops 12582912 | bytes 50331648 | tf_op jit(solution)/shard_map/stack | solution.py:129
  323.7 218.7 %while.10 = (s32[]{:T(128)}, f32[12,2048,128]{2,1,0:T(8,128)}, bf16[12,16,2,128,256]{4,3,1,0,2:T(8,128)(2,1)}, s32[12,16,128]{2,1,0:T(8,128)S(1)}, bf16[12,256,2...) while((s32[]{:T(128)}, f32[12,2048,128]{2,1,0:T(8,128)}, ...), condition=%wide.region_3.4_spmd, body=%wide.region_2.3_spmd.sunk | while | flops 1648656384 | bytes 39161648 | solution.py:130
  331.7 3.6 fusion.77
  336.6 4.4 fusion.81
  349.9 3.6 fusion.77
  354.8 4.4 fusion.81
  368.2 3.6 fusion.77
  373.0 4.4 fusion.81
  386.4 3.6 fusion.77
  391.2 4.4 fusion.81
  404.6 3.6 fusion.77
  409.5 4.4 fusion.81
  422.8 3.6 fusion.77
  427.7 4.4 fusion.81
  441.1 3.6 fusion.77
  445.9 4.4 fusion.81
  464.1 4.4 fusion.81
  482.4 4.4 fusion.81
  500.6 4.4 fusion.81
  514.0 3.6 fusion.77
  518.8 4.4 fusion.81
  537.0 4.4 fusion.81
  (165 shorter events, 141.1 us)
Async XLA Ops:
  6.5 1.8 copy-start
  9.1 10.4 %all-to-all-start = ((s32[8,2,129]{2,1,0:T(2,128)}), s32[8,2,129]{2,1,0:T(2,128)S(1)}, u32[]{:S(2)}, u32[]{:S(2)}) async-start(s32[8,2,129]{2,1,0:T(2,128)} %pad_add_fusion), calls=%async_computation | async-start | bytes 32768 | tf_op jit(solution)/shard_map/all_to_all | solution.py:13
  19.5 19.2 %all-to-all-start.1 = ((bf16[16,256,128]{2,1,0:T(8,128)(2,1)}), bf16[16,256,128]{2,1,0:T(8,128)(2,1)S(1)}, u32[]{:S(2)}, u32[]{:S(2)}) async-start(bf16[16,256,128]{2,1,0:T(8,128)(2,1)} %bitcast.48), calls=%async_computation.1 | async-start | bytes 2097152 | tf_op jit(solution)/shard_map/all_to_all | solution.py:101
  47.3 8.0 %copy-start.3 = (bf16[12,16,256]{2,1,0:T(8,128)(2,1)S(1)}, bf16[12,16,256]{2,1,0:T(8,128)(2,1)}, u32[]{:S(2)}) copy-start(bf16[12,16,256]{2,1,0:T(8,128)(2,1)} %param.11) | copy-start | bytes 294916
  47.3 8.0 %copy-start.4 = (bf16[12,16,256]{2,1,0:T(8,128)(2,1)S(1)}, bf16[12,16,256]{2,1,0:T(8,128)(2,1)}, u32[]{:S(2)}) copy-start(bf16[12,16,256]{2,1,0:T(8,128)(2,1)} %param.10) | copy-start | bytes 294916
  47.3 237.6 %all-to-all-start.2 = ((bf16[16,12,1,256,128]{3,4,1,2,0:T(8,128)(2,1)}), bf16[16,12,1,256,128]{3,4,1,2,0:T(8,128)(2,1)}, u32[]{:S(2)}, u32[]{:S(2)}) async-start(bf16[16,12,1,256,128]{3,4,1,2,0:T(8,128)(2,1)} %stack.12), calls=%async_computation.2 | async-start | bytes 25165824 | tf_op jit(solution)/shard_map/all_to_all | solution.py:118
  55.2 225.7 %all-gather.4.cloned.1.call-start = ((), (), s32[]{:S(2)}) async-start(), calls=%async_computation.3 | async-start | bytes 3342336 | tf_op jit(solution)/shard_map/all_gather | solution.py:27
  281.0 4.0 copy-start.2
  542.4 0.7 copy-start.1
Sparse Core Ops, SparseCore 0:
  58.2 198.3 all-gather.3
